TPU v7x, 32 devices: a whole 2x2x4 slice. The times are simulated.
32 devices in a mesh: gx: 4 (over z), gy: 8 (over y, x, core).
Axes of the slice: x: 2, y: 2, z: 4, core: 2. Of those that a mesh axis runs over, the one named last changes fastest.
Arguments:
- features: bfloat16 [40960, 2048], P(('gx', 'gy')), may hold values from -6 to 6
- counts: int32 [32], P(('gx', 'gy')), may hold values from 128 to 1280, as said below
- ref_mean: float32 [2048], replicated, may hold values from -6 to 6
- ref_root: float32 [2048, 2048], P('gx', 'gy'), as said below
Outputs:
- mean: float32 [2048], replicated
- root: float32 [2048, 2048], P('gx', 'gy')
- distance: float32 [], replicated
Inputs may be any that keep to these rules, and one draw needn't show every extreme that they name: Entry b counts the valid rows of shard b, which come first in it; a multiple of 128; some shard is full in every draw. `ref_root`: symmetric and positive definite.
All inputs are finite; a program needn't handle non-finite values.
Results may differ from a plain program's by a relative error of at most 0.0015.
The roundings to bfloat16 on the way count: a program that leaves them out, or rounds other values in their place, can miss the bound.
Values may be sent and summed in bfloat16 or wider, within the bound.
A program may use at most 128 MiB of HBM per device.

v0:
```python
import jax
import jax.numpy as jnp
from jax import lax
from jax.sharding import PartitionSpec as P

ITERS = 4


def product(left, right):
    left_half = left.astype(jnp.bfloat16)
    right_half = right.astype(jnp.bfloat16)
    panel = lax.all_gather(left_half, "gy", axis=1, tiled=True)
    return jnp.dot(
        panel,
        lax.all_gather(right_half, "gx", axis=0, tiled=True),
        preferred_element_type=jnp.float32,
    )


def shards(features, counts, ref_mean, ref_root):
    width = features.shape[1]
    slots = features.shape[0]
    rows_x = lax.axis_size("gx")
    cols_y = lax.axis_size("gy")
    tile_rows = width // rows_x
    tile_cols = width // cols_y
    keep = (jnp.arange(slots, dtype=jnp.int32) < counts[0])[:, None]
    masked = jnp.where(keep, features, jnp.zeros_like(features))
    partial_gram = lax.dot_general(
        masked, features, (((0,), (0,)), ((), ())), preferred_element_type=jnp.float32
    )
    column_total = jnp.sum(masked.astype(jnp.float32), axis=0)
    local_count = counts[0].astype(jnp.float32)
    total, count = lax.psum((column_total, local_count), ("gx", "gy"))
    column_block = lax.psum_scatter(partial_gram, "gy", scatter_dimension=1, tiled=True)
    gram_tile = lax.psum_scatter(column_block, "gx", scatter_dimension=0, tiled=True)
    mean = total / count
    row_start = lax.axis_index("gx") * tile_rows
    col_start = lax.axis_index("gy") * tile_cols
    mean_rows = lax.dynamic_slice_in_dim(mean, row_start, tile_rows, 0)
    mean_cols = lax.dynamic_slice_in_dim(mean, col_start, tile_cols, 0)
    cov_tile = (gram_tile - count * mean_rows[:, None] * mean_cols[None, :]) / (count - 1.0)
    row_ids = jnp.arange(tile_rows, dtype=jnp.int32) + row_start
    col_ids = jnp.arange(tile_cols, dtype=jnp.int32) + col_start
    identity_tile = (row_ids[:, None] == col_ids[None, :]).astype(jnp.float32)
    half = product(cov_tile, ref_root)
    prod = product(ref_root, half)
    square_sum, cov_trace, root_square = lax.psum(
        (jnp.sum(prod * prod), jnp.sum(cov_tile * identity_tile), jnp.sum(ref_root * ref_root)),
        ("gx", "gy"),
    )
    scale = jnp.sqrt(square_sum + 1.0)
    current = prod / scale
    partner = identity_tile
    for step in range(ITERS):
        middle = 1.5 * identity_tile - 0.5 * product(partner, current)
        current, partner = (product(current, middle), product(middle, partner))
    last_trace = lax.psum(jnp.sum(current * identity_tile), ("gx", "gy"))
    root = jnp.sqrt(scale) * current
    distance = (
        jnp.sum((mean - ref_mean) ** 2)
        + cov_trace
        + root_square
        - 2.0 * jnp.sqrt(scale) * last_trace
    ) / 64.0
    return (mean, root, distance)


def solution(mesh):
    return jax.shard_map(
        shards,
        mesh=mesh,
        in_specs=(P(("gx", "gy"), None), P(("gx", "gy")), P(), P("gx", "gy")),
        out_specs=(P(), P("gx", "gy"), P()),
        check_vma=False,
    )
```

profile of v0, /device:TPU:0, one launch (start us, length us, event | category | flops | bytes accessed | tf_op | source)
XLA Modules:
  0.0 1031.6 jit_solution(1172393237996310174)
XLA Ops:
  7.9 18.1 %fusion = f32[2048,2048]{1,0:T(8,128)} fusion(bf16[1280,2048]{1,0:T(8,128)(2,1)} %param.4, pred[1280]{0:T(1024)(128)(4,1)S(1)} %iota_compare_fusion), kind=kOutput, calls=%fused_computation.1 | convolution fusion | flops 10740039680 | bytes 22021376 | tf_op jit(solution)/shard_map/dot_general | solution.py:29
  26.1 118.8 %reduce-scatter.3.cloned.1.call-done = f32[2048,256]{1,0:T(8,128)} async-done(((f32[2048,2048]{1,0:T(8,128)}), f32[2048,256]{1,0:T(8,128)}) %reduce-scatter.3.cloned.1.call-update) | async-done | bytes 2097168 | tf_op jit(solution)/shard_map/reduce_scatter | solution.py:35
  144.9 1.4 multiply_reduce_fusion
  146.4 3.6 convert_reduce_fusion
  150.0 42.2 %all-reduce.1 = (f32[2048]{0:T(1024)S(1)}, f32[]{:T(128)}) all-reduce(f32[2048]{0:T(1024)S(1)} %convert_reduce_fusion, f32[]{:T(128)S(6)} %convert_element_type.69), channel_id=1, replica_groups=mesh['gx'=4,'gy'=8] {'gx','gy'}, use_global_device_ids=true, to_apply=%region_1.2 | all-reduce | flops 2049 | bytes 16392 | tf_op jit(solution)/shard_map/psum | solution.py:34
  192.9 1.3 multiply_reduce_fusion.2
  194.2 0.1 dynamic_slice.7
  194.3 0.7 dynamic-slice_multiply_fusion
  195.0 1.9 fusion.16
  197.0 0.5 all-gather.33.cloned.1.call-update
  197.5 23.1 %all-gather.29.cloned.1.call-done = bf16[2048,256]{1,0:T(8,128)(2,1)} async-done(((bf16[512,256]{1,0:T(8,128)(2,1)}), bf16[2048,256]{1,0:T(8,128)(2,1)}) %all-gather.29.cloned.1.call-update) | async-done | bytes 1048592 | tf_op jit(solution)/shard_map/all_gather | solution.py:15
  220.6 29.8 %all-gather.27.cloned.1.call-done = bf16[512,2048]{1,0:T(8,128)(2,1)} async-done(((bf16[512,256]{1,0:T(8,128)(2,1)}), bf16[512,2048]{1,0:T(8,128)(2,1)}) %all-gather.27.cloned.1.call-update) | async-done | bytes 2097168 | tf_op jit(solution)/shard_map/all_gather | solution.py:12
  250.4 3.3 convolution_convert_fusion.6
  253.7 0.0 all-gather.37.cloned.1.call-start
  253.8 0.8 fusion.12
  254.7 25.6 %all-gather.33.cloned.1.call-done = bf16[512,2048]{1,0:T(8,128)(2,1)} async-done(((bf16[512,256]{1,0:T(8,128)(2,1)}), bf16[512,2048]{1,0:T(8,128)(2,1)}) %all-gather.33.cloned.1.call-update) | async-done | bytes 2097168 | tf_op jit(solution)/shard_map/all_gather | solution.py:12
  280.3 30.0 %all-gather.31.cloned.1.call-done = bf16[2048,256]{1,0:T(8,128)(2,1)} async-done(((bf16[512,256]{1,0:T(8,128)(2,1)}), bf16[2048,256]{1,0:T(8,128)(2,1)}) %all-gather.31.cloned.1.call-update) | async-done | bytes 1048592 | tf_op jit(solution)/shard_map/all_gather | solution.py:15
  310.3 3.3 multiply_reduce_fusion.1
  313.6 40.4 %psum.44 = f32[]{:T(128)} all-reduce(f32[]{:T(128)} %get-tuple-element.15), channel_id=1, replica_groups=mesh['gx'=4,'gy'=8] {'gx','gy'}, use_global_device_ids=true, to_apply=%region_6.7 | all-reduce | flops 1 | bytes 8 | tf_op jit(solution)/shard_map/psum | solution.py:48
  354.7 0.7 fusion.15
  355.5 27.4 %all-gather.39.cloned.1.call-done = bf16[2048,256]{0,1:T(8,128)(2,1)} async-done(((bf16[512,256]{0,1:T(8,128)(2,1)}), bf16[2048,256]{0,1:T(8,128)(2,1)}) %all-gather.39.cloned.1.call-update) | async-done | bytes 1048592 | tf_op jit(solution)/shard_map/all_gather | solution.py:15
  383.0 3.3 fusion.8
  386.4 0.5 all-gather.35.cloned.1.call-update
  387.0 0.7 all-gather.47.cloned.1.call-update
  387.7 0.5 all-gather.45.cloned.1.call-update
  388.2 0.2 all-gather.51.cloned.1.call-start
  388.5 25.4 %all-gather.41.cloned.1.call-done = bf16[2048,256]{1,0:T(8,128)(2,1)} async-done(((bf16[512,256]{1,0:T(8,128)(2,1)}), bf16[2048,256]{1,0:T(8,128)(2,1)}) %all-gather.41.cloned.1.call-update) | async-done | bytes 1048592 | tf_op jit(solution)/shard_map/all_gather | solution.py:15
  413.8 29.5 %all-gather.35.cloned.1.call-done = bf16[512,2048]{0,1:T(8,128)(2,1)} async-done(((bf16[512,256]{0,1:T(8,128)(2,1)}), bf16[512,2048]{0,1:T(8,128)(2,1)}) %all-gather.35.cloned.1.call-update) | async-done | bytes 2097168 | tf_op jit(solution)/shard_map/all_gather | solution.py:12
  443.3 3.3 convolution_convert_fusion.5
  446.7 26.2 %all-gather.47.cloned.1.call-done = bf16[2048,256]{1,0:T(8,128)(2,1)} async-done(((bf16[512,256]{1,0:T(8,128)(2,1)}), bf16[2048,256]{1,0:T(8,128)(2,1)}) %all-gather.47.cloned.1.call-update) | async-done | bytes 1048592 | tf_op jit(solution)/shard_map/all_gather | solution.py:15
  472.9 29.2 %all-gather.45.cloned.1.call-done = bf16[512,2048]{1,0:T(8,128)(2,1)} async-done(((bf16[512,256]{1,0:T(8,128)(2,1)}), bf16[512,2048]{1,0:T(8,128)(2,1)}) %all-gather.45.cloned.1.call-update) | async-done | bytes 2097168 | tf_op jit(solution)/shard_map/all_gather | solution.py:12
  502.2 3.3 convolution_convert_fusion.4
  505.5 0.5 all-gather.43.cloned.1.call-update
  506.1 26.2 %all-gather.51.cloned.1.call-done = bf16[2048,256]{1,0:T(8,128)(2,1)} async-done(((bf16[512,256]{1,0:T(8,128)(2,1)}), bf16[2048,256]{1,0:T(8,128)(2,1)}) %all-gather.51.cloned.1.call-update) | async-done | bytes 1048592 | tf_op jit(solution)/shard_map/all_gather | solution.py:15
  532.3 29.2 %all-gather.49.cloned.1.call-done = bf16[512,2048]{1,0:T(8,128)(2,1)} async-done(((bf16[512,256]{1,0:T(8,128)(2,1)}), bf16[512,2048]{1,0:T(8,128)(2,1)}) %all-gather.49.cloned.1.call-update) | async-done | bytes 2097168 | tf_op jit(solution)/shard_map/all_gather | solution.py:12
  561.6 3.3 fusion.9
  564.9 0.5 all-gather.59.cloned.1.call-update
  565.5 0.5 all-gather.57.cloned.1.call-update
  566.1 25.9 %all-gather.43.cloned.1.call-done = bf16[512,2048]{1,0:T(8,128)(2,1)} async-done(((bf16[512,256]{1,0:T(8,128)(2,1)}), bf16[512,2048]{1,0:T(8,128)(2,1)}) %all-gather.43.cloned.1.call-update) | async-done | bytes 2097168 | tf_op jit(solution)/shard_map/all_gather | solution.py:12
  592.0 29.4 %all-gather.53.cloned.1.call-done = bf16[2048,256]{1,0:T(8,128)(2,1)} async-done(((bf16[512,256]{1,0:T(8,128)(2,1)}), bf16[2048,256]{1,0:T(8,128)(2,1)}) %all-gather.53.cloned.1.call-update) | async-done | bytes 1048592 | tf_op jit(solution)/shard_map/all_gather | solution.py:15
  621.4 3.3 convolution_convert_fusion.3
  624.8 25.5 %all-gather.59.cloned.1.call-done = bf16[2048,256]{1,0:T(8,128)(2,1)} async-done(((bf16[512,256]{1,0:T(8,128)(2,1)}), bf16[2048,256]{1,0:T(8,128)(2,1)}) %all-gather.59.cloned.1.call-update) | async-done | bytes 1048592 | tf_op jit(solution)/shard_map/all_gather | solution.py:15
  650.2 29.2 %all-gather.57.cloned.1.call-done = bf16[512,2048]{1,0:T(8,128)(2,1)} async-done(((bf16[512,256]{1,0:T(8,128)(2,1)}), bf16[512,2048]{1,0:T(8,128)(2,1)}) %all-gather.57.cloned.1.call-update) | async-done | bytes 2097168 | tf_op jit(solution)/shard_map/all_gather | solution.py:12
  679.5 3.3 convolution_convert_fusion.2
  682.8 0.7 all-gather.55.cloned.1.call-update
  683.6 26.1 %all-gather.63.cloned.1.call-done = bf16[2048,256]{1,0:T(8,128)(2,1)} async-done(((bf16[512,256]{1,0:T(8,128)(2,1)}), bf16[2048,256]{1,0:T(8,128)(2,1)}) %all-gather.63.cloned.1.call-update) | async-done | bytes 1048592 | tf_op jit(solution)/shard_map/all_gather | solution.py:15
  709.6 29.2 %all-gather.61.cloned.1.call-done = bf16[512,2048]{1,0:T(8,128)(2,1)} async-done(((bf16[512,256]{1,0:T(8,128)(2,1)}), bf16[512,2048]{1,0:T(8,128)(2,1)}) %all-gather.61.cloned.1.call-update) | async-done | bytes 2097168 | tf_op jit(solution)/shard_map/all_gather | solution.py:12
  738.9 3.3 fusion.10
  742.2 0.7 all-gather.71.cloned.1.call-update
  743.0 0.5 all-gather.69.cloned.1.call-update
  743.5 25.9 %all-gather.55.cloned.1.call-done = bf16[512,2048]{1,0:T(8,128)(2,1)} async-done(((bf16[512,256]{1,0:T(8,128)(2,1)}), bf16[512,2048]{1,0:T(8,128)(2,1)}) %all-gather.55.cloned.1.call-update) | async-done | bytes 2097168 | tf_op jit(solution)/shard_map/all_gather | solution.py:12
  769.5 29.6 %all-gather.65.cloned.1.call-done = bf16[2048,256]{1,0:T(8,128)(2,1)} async-done(((bf16[512,256]{1,0:T(8,128)(2,1)}), bf16[2048,256]{1,0:T(8,128)(2,1)}) %all-gather.65.cloned.1.call-update) | async-done | bytes 1048592 | tf_op jit(solution)/shard_map/all_gather | solution.py:15
  799.1 3.3 convolution_convert_fusion.1
  802.4 25.6 %all-gather.71.cloned.1.call-done = bf16[2048,256]{1,0:T(8,128)(2,1)} async-done(((bf16[512,256]{1,0:T(8,128)(2,1)}), bf16[2048,256]{1,0:T(8,128)(2,1)}) %all-gather.71.cloned.1.call-update) | async-done | bytes 1048592 | tf_op jit(solution)/shard_map/all_gather | solution.py:15
  828.0 29.2 %all-gather.69.cloned.1.call-done = bf16[512,2048]{1,0:T(8,128)(2,1)} async-done(((bf16[512,256]{1,0:T(8,128)(2,1)}), bf16[512,2048]{1,0:T(8,128)(2,1)}) %all-gather.69.cloned.1.call-update) | async-done | bytes 2097168 | tf_op jit(solution)/shard_map/all_gather | solution.py:12
  857.3 3.3 convolution_convert_fusion
  860.6 0.5 all-gather.67.cloned.1.call-update
  861.2 26.2 %all-gather.75.cloned.1.call-done = bf16[2048,256]{1,0:T(8,128)(2,1)} async-done(((bf16[512,256]{1,0:T(8,128)(2,1)}), bf16[2048,256]{1,0:T(8,128)(2,1)}) %all-gather.75.cloned.1.call-update) | async-done | bytes 1048592 | tf_op jit(solution)/shard_map/all_gather | solution.py:15
  887.4 29.2 %all-gather.73.cloned.1.call-done = bf16[512,2048]{1,0:T(8,128)(2,1)} async-done(((bf16[512,256]{1,0:T(8,128)(2,1)}), bf16[512,2048]{1,0:T(8,128)(2,1)}) %all-gather.73.cloned.1.call-update) | async-done | bytes 2097168 | tf_op jit(solution)/shard_map/all_gather | solution.py:12
  916.7 3.3 fusion.11
  920.0 27.1 %all-gather.67.cloned.1.call-done = bf16[512,2048]{1,0:T(8,128)(2,1)} async-done(((bf16[512,256]{1,0:T(8,128)(2,1)}), bf16[512,2048]{1,0:T(8,128)(2,1)}) %all-gather.67.cloned.1.call-update) | async-done | bytes 2097168 | tf_op jit(solution)/shard_map/all_gather | solution.py:12
  947.1 29.6 %all-gather.77.cloned.1.call-done = bf16[2048,256]{1,0:T(8,128)(2,1)} async-done(((bf16[512,256]{1,0:T(8,128)(2,1)}), bf16[2048,256]{1,0:T(8,128)(2,1)}) %all-gather.77.cloned.1.call-update) | async-done | bytes 1048592 | tf_op jit(solution)/shard_map/all_gather | solution.py:15
  976.7 4.0 fusion.14
  980.7 40.4 %all-reduce = (f32[]{:T(128)}, f32[]{:T(128)}, f32[]{:T(128)}) all-reduce(f32[]{:T(128)} %get-tuple-element.4, f32[]{:T(128)} %get-tuple-element.12, f32[]{:T(128)} %get-tuple-element.3), channel_id=1, replica_groups=mesh['gx'=4,'gy'=8] {'gx','gy'}, use_global_device_ids=true, to_apply=%region_9.10 | all-reduce | flops 3 | bytes 24 | tf_op jit(solution)/shard_map/psum | solution.py:48
  (56 shorter events, 1.4 us)
Async XLA Ops:
  7.2 137.7 %reduce-scatter.3.cloned.1.call-start = ((), (), s32[]{:S(2)}) async-start(), calls=%async_computation.2 | async-start | bytes 18874368 | tf_op jit(solution)/shard_map/reduce_scatter | solution.py:35
  26.0 118.9 %copy-start = (f32[512,256]{1,0:T(8,128)S(1)}, f32[512,256]{1,0:T(8,128)}, u32[]{:S(2)}) copy-start(f32[512,256]{1,0:T(8,128)} %param.7) | copy-start | bytes 1572868
  26.0 169.0 %reduce-scatter.5.cloned.1.call-start = ((), (), s32[]{:S(2)}) async-start(), calls=%async_computation.3 | async-start | bytes 2621440 | tf_op jit(solution)/shard_map/reduce_scatter | solution.py:36
  144.8 75.8 %all-gather.29.cloned.1.call-start = ((), (), s32[]{:S(2)}) async-start(), calls=%async_computation.5 | async-start | bytes 1310720 | tf_op jit(solution)/shard_map/all_gather | solution.py:15
  146.3 104.1 %all-gather.27.cloned.1.call-start = ((), (), s32[]{:S(2)}) async-start(), calls=%async_computation.4 | async-start | bytes 2359296 | tf_op jit(solution)/shard_map/all_gather | solution.py:12
  146.4 46.5 %copy-start.3 = (f32[2048]{0:T(1024)S(1)}, f32[2048]{0:T(1024)}, u32[]{:S(2)}) copy-start(f32[2048]{0:T(1024)} %param.6) | copy-start | bytes 24580
  194.2 59.5 %copy-start.2 = (f32[2048]{0:T(1024)}, f32[2048]{0:T(1024)S(1)}, u32[]{:S(2)}) copy-start(f32[2048]{0:T(1024)S(1)} %get-tuple-element.11) | copy-start | bytes 24580
  196.9 83.4 %all-gather.33.cloned.1.call-start = ((), (), s32[]{:S(2)}) async-start(), calls=%async_computation.7 | async-start | bytes 2359296 | tf_op jit(solution)/shard_map/all_gather | solution.py:12
  197.5 112.8 %all-gather.31.cloned.1.call-start = ((), (), s32[]{:S(2)}) async-start(), calls=%async_computation.6 | async-start | bytes 1310720 | tf_op jit(solution)/shard_map/all_gather | solution.py:15
  253.7 101.8 %all-gather.37.cloned.1.call-start = ((), (), s32[]{:S(2)}) async-start(), calls=%async_computation.9 | async-start | bytes 2359296 | tf_op jit(solution)/shard_map/all_gather | solution.py:12
  254.7 128.3 %all-gather.39.cloned.1.call-start = ((), (), s32[]{:S(2)}) async-start(), calls=%async_computation.10 | async-start | bytes 1310720 | tf_op jit(solution)/shard_map/all_gather | solution.py:15
  355.5 58.4 %all-gather.41.cloned.1.call-start = ((), (), s32[]{:S(2)}) async-start(), calls=%async_computation.11 | async-start | bytes 1310720 | tf_op jit(solution)/shard_map/all_gather | solution.py:15
  386.3 57.0 %all-gather.35.cloned.1.call-start = ((), (), s32[]{:S(2)}) async-start(), calls=%async_computation.8 | async-start | bytes 2359296 | tf_op jit(solution)/shard_map/all_gather | solution.py:12
  386.9 86.0 %all-gather.47.cloned.1.call-start = ((), (), s32[]{:S(2)}) async-start(), calls=%async_computation.14 | async-start | bytes 1310720 | tf_op jit(solution)/shard_map/all_gather | solution.py:15
  387.7 114.5 %all-gather.45.cloned.1.call-start = ((), (), s32[]{:S(2)}) async-start(), calls=%async_computation.13 | async-start | bytes 2359296 | tf_op jit(solution)/shard_map/all_gather | solution.py:12
  388.2 144.1 %all-gather.51.cloned.1.call-start = ((), (), s32[]{:S(2)}) async-start(), calls=%async_computation.16 | async-start | bytes 1310720 | tf_op jit(solution)/shard_map/all_gather | solution.py:15
  446.7 114.9 %all-gather.49.cloned.1.call-start = ((), (), s32[]{:S(2)}) async-start(), calls=%async_computation.15 | async-start | bytes 2359296 | tf_op jit(solution)/shard_map/all_gather | solution.py:12
  505.5 86.5 %all-gather.43.cloned.1.call-start = ((), (), s32[]{:S(2)}) async-start(), calls=%async_computation.12 | async-start | bytes 2359296 | tf_op jit(solution)/shard_map/all_gather | solution.py:12
  506.1 115.4 %all-gather.53.cloned.1.call-start = ((), (), s32[]{:S(2)}) async-start(), calls=%async_computation.17 | async-start | bytes 1310720 | tf_op jit(solution)/shard_map/all_gather | solution.py:15
  564.9 85.4 %all-gather.59.cloned.1.call-start = ((), (), s32[]{:S(2)}) async-start(), calls=%async_computation.20 | async-start | bytes 1310720 | tf_op jit(solution)/shard_map/all_gather | solution.py:15
  565.5 114.0 %all-gather.57.cloned.1.call-start = ((), (), s32[]{:S(2)}) async-start(), calls=%async_computation.19 | async-start | bytes 2359296 | tf_op jit(solution)/shard_map/all_gather | solution.py:12
  566.0 143.6 %all-gather.63.cloned.1.call-start = ((), (), s32[]{:S(2)}) async-start(), calls=%async_computation.22 | async-start | bytes 1310720 | tf_op jit(solution)/shard_map/all_gather | solution.py:15
  624.7 114.1 %all-gather.61.cloned.1.call-start = ((), (), s32[]{:S(2)}) async-start(), calls=%async_computation.21 | async-start | bytes 2359296 | tf_op jit(solution)/shard_map/all_gather | solution.py:12
  682.8 86.7 %all-gather.55.cloned.1.call-start = ((), (), s32[]{:S(2)}) async-start(), calls=%async_computation.18 | async-start | bytes 2359296 | tf_op jit(solution)/shard_map/all_gather | solution.py:12
  683.5 115.5 %all-gather.65.cloned.1.call-start = ((), (), s32[]{:S(2)}) async-start(), calls=%async_computation.23 | async-start | bytes 1310720 | tf_op jit(solution)/shard_map/all_gather | solution.py:15
  742.2 85.8 %all-gather.71.cloned.1.call-start = ((), (), s32[]{:S(2)}) async-start(), calls=%async_computation.26 | async-start | bytes 1310720 | tf_op jit(solution)/shard_map/all_gather | solution.py:15
  742.9 114.3 %all-gather.69.cloned.1.call-start = ((), (), s32[]{:S(2)}) async-start(), calls=%async_computation.25 | async-start | bytes 2359296 | tf_op jit(solution)/shard_map/all_gather | solution.py:12
  743.5 143.9 %all-gather.75.cloned.1.call-start = ((), (), s32[]{:S(2)}) async-start(), calls=%async_computation.28 | async-start | bytes 1310720 | tf_op jit(solution)/shard_map/all_gather | solution.py:15
  802.3 114.3 %all-gather.73.cloned.1.call-start = ((), (), s32[]{:S(2)}) async-start(), calls=%async_computation.27 | async-start | bytes 2359296 | tf_op jit(solution)/shard_map/all_gather | solution.py:12
  860.5 86.5 %all-gather.67.cloned.1.call-start = ((), (), s32[]{:S(2)}) async-start(), calls=%async_computation.24 | async-start | bytes 2359296 | tf_op jit(solution)/shard_map/all_gather | solution.py:12
  861.1 115.5 %copy-start.1 = (f32[512,256]{1,0:T(8,128)S(1)}, f32[512,256]{1,0:T(8,128)}, u32[]{:S(2)}) copy-start(f32[512,256]{1,0:T(8,128)} %reduce-scatter.5.cloned.1.call-done) | copy-start | bytes 1572868
  861.2 115.5 %all-gather.77.cloned.1.call-start = ((), (), s32[]{:S(2)}) async-start(), calls=%async_computation.29 | async-start | bytes 1310720 | tf_op jit(solution)/shard_map/all_gather | solution.py:15
Sparse Core Ops, SparseCore 0:
  26.1 118.6 reduce-scatter.2
  147.1 44.6 reduce-scatter.4
  193.4 27.1 all-gather.28
  222.9 27.4 all-gather.26
  252.2 28.0 all-gather.32
  282.3 27.9 all-gather.30
  312.2 27.6 all-gather.36
  355.6 27.3 all-gather.38
  386.5 27.3 all-gather.40
  416.2 27.1 all-gather.34
  444.9 27.9 all-gather.46
  474.7 27.4 all-gather.44
  504.3 27.9 all-gather.50
  534.1 27.4 all-gather.48
  563.9 28.0 all-gather.42
  593.4 27.9 all-gather.52
  622.9 27.3 all-gather.58
  652.0 27.4 all-gather.56
  681.6 27.9 all-gather.62
  711.4 27.4 all-gather.60
  741.3 28.0 all-gather.54
  771.0 27.9 all-gather.64
  800.6 27.3 all-gather.70
  829.8 27.4 all-gather.68
  859.4 27.9 all-gather.74
  889.1 27.4 all-gather.72
  919.0 28.0 all-gather.66
  948.7 27.9 all-gather.76
where the time goes:
time: 1030 us
  waiting for transfers between devices  815 us (79%)
  blocking collectives  123 us (12%)
  matrix products  61.5 us (6%)
  between operations  20.3 us (2%)
  other arithmetic  10.5 us (1%)
    all_gather x13, waiting for transfers between devices, product(): lax.all_gather(right_half, 'gx', axis=0, tiled=True)  350 us
    all_gather x13, waiting for transfers between devices, product(): panel = lax.all_gather(left_half, 'gy', axis=1, tiled=True)  339 us
    reduce_scatter x1, waiting for transfers between devices, shards(): lax.psum_scatter(partial_gram, 'gy', scatter_dimension=1, tiled=True)  119 us
    psum x2, blocking collectives, shards(): lax.psum((jnp.sum(prod * prod), jnp.sum(cov_tile * identity_tile), jnp.su...  80.7 us
    dot_general x13, matrix products, product(): jnp.dot(panel, lax.all_gather(right_half, 'gx', axis=0, tiled=True), pref...  43.4 us
    psum x1, blocking collectives, shards(): total, count = lax.psum((column_total, local_count), ('gx', 'gy'))  42.2 us
  transfers between devices with their start and end apart: 28, of which 26 were waited for; matrix products, arithmetic and copies ran while one was open for 5% of the time, Pallas kernels for 0%

commit v1 on v0

v1 whole, which is shorter than its diff:
```python
import functools

import jax
import jax.numpy as jnp
from jax import lax
from jax.experimental import pallas as pl
from jax.experimental.pallas import tpu as pltpu
from jax.sharding import PartitionSpec as P

MESH = pl.DeviceIdType.MESH
F32 = jnp.float32
BF16 = jnp.bfloat16


def dot(a, b):
    return jnp.dot(a, b, preferred_element_type=F32)


def chain_kernel(nx, ny, bm, bn, cov_ref, root_ref, part_ref, tile_ref, sums_ref,
                 a, b, c, e, f, prod, ycol, wcol, acc, norm, slots, load_sem, send, recv,
                 norm_send, norm_recv, sum_send, sum_recv):
    width = a.shape[0]
    half = width // 2
    chunks = width // bm
    tr, tc = width // nx, width // ny
    mx, my = lax.axis_index("gx"), lax.axis_index("gy")
    mine = lax.rem(my, 2)
    partner = (mx, my + 1 - 2 * mine)
    col0 = pl.multiple_of(mine * half, half)
    cols = pl.ds(col0, half)

    def load(k, src, dst, s):
        i, j = k // ny, lax.rem(k, ny)
        return pltpu.make_async_copy(
            src.at[pl.ds(pl.multiple_of(k * tr, tr), tr), :],
            dst.at[pl.ds(pl.multiple_of(i * tr, tr), tr), pl.ds(pl.multiple_of(j * tc, tc), tc)],
            load_sem.at[s, k])

    @pl.loop(0, nx * ny)
    def _(k):
        load(k, cov_ref, c, 0).start()
        load(k, root_ref, b, 1).start()

    barrier = pltpu.get_barrier_semaphore()

    def other(d):
        q = d + 1
        return lax.rem(mx + q // ny, nx), lax.rem(my + lax.rem(q, ny), ny)

    def source(d):
        q = d + 1
        return lax.rem(mx + nx - q // ny, nx), lax.rem(my + ny - lax.rem(q, ny), ny)

    @pl.loop(0, nx * ny - 1)
    def _(d):
        pl.semaphore_signal(barrier, inc=1, device_id=other(d), device_id_type=MESH)
    pl.semaphore_wait(barrier, nx * ny - 1)

    @pl.loop(0, nx * ny)
    def _(k):
        load(k, cov_ref, c, 0).wait()
        load(k, root_ref, b, 1).wait()

    def rows_of(k):
        return pl.ds(pl.multiple_of(k * bm, bm), bm)

    def copy(buf, s, k):
        return pltpu.make_async_remote_copy(
            src_ref=buf.at[rows_of(k), cols], dst_ref=buf.at[rows_of(k), cols],
            send_sem=send.at[s, k], recv_sem=recv.at[s, k],
            device_id=partner, device_id_type=MESH)

    def arrived(buf, s, k):
        copy(buf, s, k).wait()

    def blocks(k, left, right, put):
        @pl.loop(0, half // bn)
        def _(n):
            cs = pl.ds(pl.multiple_of(col0 + n * bn, bn), bn)
            put(k, n, cs, dot(left[rows_of(k), :], right[:, cs]))

    def diag(r0, c0, shape):
        r = lax.broadcasted_iota(jnp.int32, shape, 0) + r0
        q = lax.broadcasted_iota(jnp.int32, shape, 1) + c0
        return r == q

    def middle(t, r0, c0):
        return jnp.where(diag(r0, c0, t.shape), 1.5, 0.0) - 0.5 * t

    @pl.loop(0, chunks)
    def _(k):
        def put(k, n, cs, v):
            e[rows_of(k), cs] = v.astype(BF16)
        blocks(k, c, b, put)

    acc[...] = jnp.zeros_like(acc)

    @pl.loop(0, chunks)
    def _(k):
        def put(k, n, cs, v):
            prod[rows_of(k), pl.ds(pl.multiple_of(n * bn, bn), bn)] = v
            acc[...] += jnp.sum((v * v).reshape(bm // 8, 8, bn), axis=0)
        blocks(k, b, e, put)
    norm[0] = jnp.full((8, 128), jnp.sum(acc[...]), F32)
    swap = pltpu.make_async_remote_copy(
        src_ref=norm.at[0], dst_ref=norm.at[1], send_sem=norm_send, recv_sem=norm_recv,
        device_id=partner, device_id_type=MESH)
    swap.start()
    swap.wait()
    scale = jnp.sqrt(norm[0] + norm[1] + 1.0)
    scale_one = scale[0:1, 0:1]

    @pl.loop(0, chunks)
    def _(k):
        @pl.loop(0, half // bn)
        def _(n):
            cs = pl.ds(pl.multiple_of(col0 + n * bn, bn), bn)
            y = (prod[rows_of(k), pl.ds(pl.multiple_of(n * bn, bn), bn)] / scale_one).astype(BF16)
            a[rows_of(k), cs] = y
            b[rows_of(k), cs] = middle(y.astype(F32), k * bm, col0 + n * bn).astype(BF16)
        copy(a, 0, k).start()
        copy(b, 1, k).start()

    def stage(left, right, out, wait, s, mid=False):
        @pl.loop(0, chunks)
        def _(k):
            for buf, w in wait:
                arrived(buf, w, k)

            def put(k, n, cs, v):
                if mid:
                    v = middle(v, k * bm, col0 + n * bn)
                out[rows_of(k), cs] = v.astype(BF16)
            blocks(k, left, right, put)
            copy(out, s, k).start()

    stage(a, b, e, [(a, 0)], 2)
    stage(b, e, c, [(b, 1)], 3, True)
    stage(c, b, f, [(c, 3)], 4)
    stage(e, c, a, [(e, 2)], 5)
    stage(f, a, b, [(f, 4)], 6, True)
    stage(b, f, e, [(b, 6)], 7)

    @pl.loop(0, chunks)
    def _(k):
        arrived(a, 5, k)

    my_rows = pl.ds(pl.multiple_of(mx * tr, tr), tr)
    my_cols = pl.ds(pl.multiple_of(my * tc, tc), tc)

    @pl.loop(0, width // bn)
    def _(n):
        cs = pl.ds(pl.multiple_of(n * bn, bn), bn)
        c[pl.ds(0, tr), cs] = dot(a[my_rows, :], b[:, cs]).astype(BF16)

    @pl.loop(0, chunks)
    def _(k):
        ycol[rows_of(k), :] = dot(a[rows_of(k), :], b[:, my_cols]).astype(BF16)

    @pl.loop(0, chunks)
    def _(k):
        arrived(e, 7, k)
        t = dot(e[rows_of(k), :], ycol[...])
        wcol[rows_of(k), :] = middle(t, k * bm, my * tc).astype(BF16)

    last = dot(c[pl.ds(0, tr), :], wcol[...])
    tile_ref[...] = last
    trace = jnp.sum(jnp.where(diag(mx * tr, my * tc, last.shape), last, 0.0))
    line = lax.broadcasted_iota(jnp.int32, (8, 128), 0)
    me = mx * ny + my
    slots[me] = part_ref[...] + jnp.where(line == 2, trace, 0.0)

    def share(dev, slot):
        return pltpu.make_async_remote_copy(
            src_ref=slots.at[slot], dst_ref=slots.at[slot],
            send_sem=sum_send.at[slot], recv_sem=sum_recv.at[slot],
            device_id=dev, device_id_type=MESH)

    def share_to(d):
        ox, oy = other(d)
        return pltpu.make_async_remote_copy(
            src_ref=slots.at[me], dst_ref=slots.at[me],
            send_sem=sum_send.at[ox * ny + oy], recv_sem=sum_recv.at[me],
            device_id=(ox, oy), device_id_type=MESH)

    @pl.loop(0, nx * ny - 1)
    def _(d):
        share_to(d).start()

    @pl.loop(0, nx * ny - 1)
    def _(d):
        sx, sy = source(d)
        share((sx, sy), sx * ny + sy).wait_recv()

    @pl.loop(0, nx * ny - 1)
    def _(d):
        share_to(d).wait_send()
    sums_ref[...] = jnp.sum(slots[...], axis=0) + jnp.where(line == 3, scale, 0.0)


def chain(nx, ny, cov_tiles, root_tiles, part):
    width = nx * (cov_tiles.shape[0] // (nx * ny))
    half = width // 2
    tr, tc = width // nx, width // ny
    bm, bn = 512, 512
    chunks = width // bm
    n = nx * ny
    return pl.pallas_call(
        functools.partial(chain_kernel, nx, ny, bm, bn),
        name="chain",
        out_shape=(jax.ShapeDtypeStruct((tr, tc), F32), jax.ShapeDtypeStruct((8, 128), F32)),
        in_specs=[pl.BlockSpec(memory_space=pl.ANY)] * 2 + [pl.BlockSpec(memory_space=pltpu.VMEM)],
        out_specs=(pl.BlockSpec(memory_space=pltpu.VMEM), pl.BlockSpec(memory_space=pltpu.VMEM)),
        scratch_shapes=[pltpu.VMEM((width, width), BF16)] * 5 + [
            pltpu.VMEM((width, half), F32),
            pltpu.VMEM((width, tc), BF16),
            pltpu.VMEM((width, tc), BF16),
            pltpu.VMEM((8, bn), F32),
            pltpu.VMEM((2, 8, 128), F32),
            pltpu.VMEM((n, 8, 128), F32),
            pltpu.SemaphoreType.DMA((2, n)),
            pltpu.SemaphoreType.DMA((8, chunks)),
            pltpu.SemaphoreType.DMA((8, chunks)),
            pltpu.SemaphoreType.DMA,
            pltpu.SemaphoreType.DMA,
            pltpu.SemaphoreType.DMA((n,)),
            pltpu.SemaphoreType.DMA((n,)),
        ],
        compiler_params=pltpu.CompilerParams(
            collective_id=0, has_side_effects=True, vmem_limit_bytes=62 * 2**20),
    )(cov_tiles, root_tiles, part)


def shards(nx, ny, features, counts, ref_mean, ref_root):
    width = features.shape[1]
    slots = features.shape[0]
    tile_rows = width // nx
    tile_cols = width // ny
    both = ("gx", "gy")
    root_tiles = lax.all_gather(ref_root.astype(BF16), both, axis=0, tiled=True)
    keep = (jnp.arange(slots, dtype=jnp.int32) < counts[0])[:, None]
    masked = jnp.where(keep, features, jnp.zeros_like(features))
    partial_gram = lax.dot_general(
        masked, features, (((0,), (0,)), ((), ())), preferred_element_type=F32
    )
    column_total = jnp.sum(masked.astype(F32), axis=0)
    local_count = counts[0].astype(F32)
    total, count = lax.psum((column_total, local_count), both)
    column_block = lax.psum_scatter(partial_gram, "gy", scatter_dimension=1, tiled=True)
    gram_tile = lax.psum_scatter(column_block, "gx", scatter_dimension=0, tiled=True)
    mean = total / count
    row_start = lax.axis_index("gx") * tile_rows
    col_start = lax.axis_index("gy") * tile_cols
    mean_rows = lax.dynamic_slice_in_dim(mean, row_start, tile_rows, 0)
    mean_cols = lax.dynamic_slice_in_dim(mean, col_start, tile_cols, 0)
    cov_tile = (gram_tile - count * mean_rows[:, None] * mean_cols[None, :]) / (count - 1.0)
    row_ids = jnp.arange(tile_rows, dtype=jnp.int32) + row_start
    col_ids = jnp.arange(tile_cols, dtype=jnp.int32) + col_start
    on_diag = row_ids[:, None] == col_ids[None, :]
    cov_tiles = lax.all_gather(cov_tile.astype(BF16), both, axis=0, tiled=True)
    line = lax.broadcasted_iota(jnp.int32, (8, 128), 0)
    part = jnp.where(
        line == 0, jnp.sum(jnp.where(on_diag, cov_tile, 0.0)),
        jnp.where(line == 1, jnp.sum(ref_root * ref_root), 0.0))
    tile, sums = chain(nx, ny, cov_tiles, root_tiles, part)
    scale = sums[3, 0]
    root = jnp.sqrt(scale) * tile
    distance = (
        jnp.sum((mean - ref_mean) ** 2) + sums[0, 0] + sums[1, 0]
        - 2.0 * jnp.sqrt(scale) * sums[2, 0]
    ) / 64.0
    return (mean, root, distance)


def solution(mesh):
    return jax.shard_map(
        functools.partial(shards, mesh.shape["gx"], mesh.shape["gy"]),
        mesh=mesh,
        in_specs=(P(("gx", "gy"), None), P(("gx", "gy")), P(), P("gx", "gy")),
        out_specs=(P(), P("gx", "gy"), P()),
        check_vma=False,
    )
```

time: 1030 us -> 461 us (0.45)
  waiting for transfers between devices: 815 us -> 250 us
  Pallas kernels: 0 us -> 114 us
  blocking collectives: 123 us -> 42.5 us
  matrix products: 61.5 us -> 18.2 us
    all_gather x26 -> x2, waiting for transfers between devices: 690 us -> 131 us  [the longest x1 78.9 us: shards(): cov_tiles = lax.all_gather(cov_tile.astype(BF16), both, axis=0, tiled=True)]
    pallas_call x0 -> x1, Pallas kernels: none -> 114 us  [chain(): pl.pallas_call(functools.partial(chain_kernel, nx, ny, bm, bn), name='cha...]
    psum x3 -> x1, blocking collectives: 123 us -> 42.5 us  [shards(): total, count = lax.psum((column_total, local_count), both)]
    dot_general x13 -> x0, matrix products: 43.4 us -> none  [product(): jnp.dot(panel, lax.all_gather(right_half, 'gx', axis=0, tiled=True), pref...]
  transfers between devices with their start and end apart: 28 -> 4, of which waited for: 26 -> 4; matrix products, arithmetic and copies ran while one was open for 5% -> 2% of each run, Pallas kernels for 0% -> 0%
where the time goes in v1:
time: 461 us
  waiting for transfers between devices  250 us (54%)
  Pallas kernels  114 us (25%)
  blocking collectives  42.5 us (9%)
  between operations  21.2 us (5%)
  matrix products  18.2 us (4%)
  other arithmetic  13.2 us (3%)
    reduce_scatter x1, waiting for transfers between devices, shards(): lax.psum_scatter(partial_gram, 'gy', scatter_dimension=1, tiled=True)  119 us
    pallas_call x1, Pallas kernels, chain(): pl.pallas_call(functools.partial(chain_kernel, nx, ny, bm, bn), name='cha...  114 us
    all_gather x1, waiting for transfers between devices, shards(): cov_tiles = lax.all_gather(cov_tile.astype(BF16), both, axis=0, tiled=True)  78.9 us
    all_gather x1, waiting for transfers between devices, shards(): root_tiles = lax.all_gather(ref_root.astype(BF16), both, axis=0, tiled=True)  51.7 us
    psum x1, blocking collectives, shards(): total, count = lax.psum((column_total, local_count), both)  42.5 us
    dot_general x1, matrix products, shards(): lax.dot_general(masked, features, (((0,), (0,)), ((), ())), preferred_ele...  18.2 us
  transfers between devices with their start and end apart: 4, of which 4 were waited for; matrix products, arithmetic and copies ran while one was open for 2% of the time, Pallas kernels for 0%

profile of v1, /device:TPU:0, one launch (start us, length us, event | category | flops | bytes accessed | tf_op | source)
XLA Modules:
  0.0 460.9 jit_solution(15956215819921357448)
XLA Ops:
  8.0 0.0 reduce-scatter.3.cloned.1.call-start
  8.7 18.2 %fusion = f32[2048,2048]{1,0:T(8,128)} fusion(bf16[1280,2048]{1,0:T(8,128)(2,1)} %param.4, pred[1280]{0:T(1024)(128)(4,1)S(1)} %iota_compare_fusion), kind=kOutput, calls=%fused_computation.1 | convolution fusion | flops 10740039680 | bytes 22021376 | tf_op jit(solution)/shard_map/dot_general | solution.py:243
  26.9 0.0 copy-start
  26.9 0.0 reduce-scatter.3.cloned.1.call-update
  26.9 0.0 copy-start.2
  26.9 0.0 reduce-scatter.5.cloned.1.call-start
  27.0 118.8 %reduce-scatter.3.cloned.1.call-done = f32[2048,256]{1,0:T(8,128)} async-done(((f32[2048,2048]{1,0:T(8,128)}), f32[2048,256]{1,0:T(8,128)}) %reduce-scatter.3.cloned.1.call-update) | async-done | bytes 2097168 | tf_op jit(solution)/shard_map/reduce_scatter | solution.py:249
  145.7 0.0 reduce-scatter.5.cloned.1.call-update
  145.8 0.0 all-gather.5.cloned.1.call-start
  145.8 0.0 copy-done
  145.8 1.4 multiply_reduce_fusion
  147.2 0.0 all-gather.5.cloned.1.call-update
  147.2 0.0 all-gather.3.cloned.1.call-start
  147.3 3.6 convert_reduce_fusion
  150.9 42.5 %all-reduce = (f32[2048]{0:T(1024)S(1)}, f32[]{:T(128)}) all-reduce(f32[2048]{0:T(1024)S(1)} %convert_reduce_fusion, f32[]{:T(128)S(6)} %convert_element_type.13), channel_id=1, replica_groups=mesh['gx'=4,'gy'=8] {'gx','gy'}, use_global_device_ids=true, to_apply=%region_1.2 | all-reduce | flops 2049 | bytes 16392 | tf_op jit(solution)/shard_map/psum | solution.py:248
  194.1 0.0 copy-done.2
  194.1 1.2 multiply_reduce_fusion.1
  195.3 0.0 copy-start.1
  195.3 0.1 dynamic_slice.7
  195.4 0.7 dynamic-slice_multiply_fusion
  196.1 0.7 reduce-scatter.5.cloned.1.call-done
  196.8 2.6 select_reduce_fusion
  199.4 0.0 all-gather.3.cloned.1.call-update
  199.4 0.6 compare_select_fusion
  200.0 1.3 broadcast_select_fusion.part_ref
  201.3 51.7 %all-gather.5.cloned.1.call-done.root_ref = bf16[16384,256]{1,0:T(8,128)(2,1)} async-done(((bf16[512,256]{1,0:T(8,128)(2,1)}), bf16[16384,256]{1,0:T(8,128)(2,1)}) %all-gather.5.cloned.1.call-update) | async-done | bytes 8388624 | tf_op jit(solution)/shard_map/all_gather | solution.py:240
  253.0 78.9 %all-gather.3.cloned.1.call-done.cov_ref = bf16[16384,256]{1,0:T(8,128)(2,1)} async-done(((bf16[512,256]{1,0:T(8,128)(2,1)}), bf16[16384,256]{1,0:T(8,128)(2,1)}) %all-gather.3.cloned.1.call-update) | async-done | bytes 8388624 | tf_op jit(solution)/shard_map/all_gather | solution.py:260
  331.9 113.9 %chain.1 = (f32[512,256]{1,0:T(8,128)}, f32[8,128]{1,0:T(8,128)}) custom-call(bf16[16384,256]{1,0:T(8,128)(2,1)} %all-gather.3.cloned.1.call-done.cov_ref, bf16[16384,256]{1,0:T(8,128)(2,1)} %all-gather.5.cloned.1.call-done.root_ref, f32[8,128]{1,0:T(8,128)} %broadcast_select_fusion.part_ref), custom_call_target="tpu_custom_call" | custom-call | tf_op jit(solution)/shard_map/chain/pallas_call | solution.py:208
  445.8 0.0 copy-done.1
  445.9 1.4 fusion.6
  448.0 1.9 broadcast_multiply_fusion
  (4 shorter events, 0.0 us)
Async XLA Ops:
  8.0 137.8 %reduce-scatter.3.cloned.1.call-start = ((), (), s32[]{:S(2)}) async-start(), calls=%async_computation.2 | async-start | bytes 18874368 | tf_op jit(solution)/shard_map/reduce_scatter | solution.py:249
  26.9 118.9 %copy-start = (f32[512,256]{1,0:T(8,128)S(1)}, f32[512,256]{1,0:T(8,128)}, u32[]{:S(2)}) copy-start(f32[512,256]{1,0:T(8,128)} %param.7) | copy-start | bytes 1572868
  26.9 167.2 %copy-start.2 = (f32[2048]{0:T(1024)S(1)}, f32[2048]{0:T(1024)}, u32[]{:S(2)}) copy-start(f32[2048]{0:T(1024)} %param.6) | copy-start | bytes 24580
  26.9 169.9 %reduce-scatter.5.cloned.1.call-start = ((), (), s32[]{:S(2)}) async-start(), calls=%async_computation.3 | async-start | bytes 2621440 | tf_op jit(solution)/shard_map/reduce_scatter | solution.py:250
  145.8 107.3 %all-gather.5.cloned.1.call-start = ((), (), s32[]{:S(2)}) async-start(), calls=%async_computation.5 | async-start | bytes 8650752 | tf_op jit(solution)/shard_map/all_gather | solution.py:240
  147.2 184.7 %all-gather.3.cloned.1.call-start = ((), (), s32[]{:S(2)}) async-start(), calls=%async_computation.4 | async-start | bytes 8650752 | tf_op jit(solution)/shard_map/all_gather | solution.py:260
  195.3 250.5 %copy-start.1 = (f32[2048]{0:T(1024)}, f32[2048]{0:T(1024)S(1)}, u32[]{:S(2)}) copy-start(f32[2048]{0:T(1024)S(1)} %get-tuple-element.10) | copy-start | bytes 24580
Sparse Core Ops, SparseCore 0:
  27.0 118.6 reduce-scatter.2
  148.0 48.7 reduce-scatter.4
Sparse Core Ops, SparseCore 1:
  149.1 103.9 all-gather.4
  256.4 75.5 all-gather.2
